TPU v7x, 512 devices: a 4x2x32 block of a 4x8x32 slice. The times are simulated.
512 devices in a mesh: crops: 2 (over y), dap: 64 (over z, core), chan: 4 (over x).
Axes of the slice: x: 4, y: 2, z: 32, core: 2. Of those that a mesh axis runs over, the one named last changes fastest.
The devices are a block of a 4x8x32 slice.
Arguments:
- prior_pair: bfloat16 [512, 256, 128], P(('crops', 'dap')), parts along dimension 0, may hold values from -12 to 12
- single: bfloat16 [512, 384], P(('crops', 'dap')), parts along dimension 0, may hold values from -6 to 6
- target: int32 [512], P(('crops', 'dap')), parts along dimension 0, may hold values from 0 to 21
- residue_mask: int32 [512], P(('crops', 'dap')), parts along dimension 0, may hold values 0 or 1
- recycle_gain: float32 [128], replicated, may hold values from 0.5 to 1.5
- recycle_bias: float32 [128], replicated, may hold values from -3 to 3
- left_single: bfloat16 [384, 128], replicated, may hold values from -0.3125 to 0.3125
- right_single: bfloat16 [384, 128], replicated, may hold values from -0.3125 to 0.3125
- left_target: bfloat16 [22, 128], replicated, may hold values from -3 to 3
- right_target: bfloat16 [22, 128], replicated, may hold values from -3 to 3
- tri_gain: float32 [2, 128], replicated, may hold values from 0.25 to 1.75
- tri_proj: bfloat16 [2, 128, 4, 128], replicated, may hold values from -0.5 to 0.5
- tri_gate: bfloat16 [2, 128, 128], replicated, may hold values from -0.5 to 0.5
- tri_gate_bias: float32 [2, 128], replicated, may hold values from -4 to 4
- tri_out_gain: float32 [2, 128], replicated, may hold values from 0.25 to 1.75
- tri_out: bfloat16 [2, 128, 128], replicated, may hold values from -0.5 to 0.5
Outputs:
- updated_pair: bfloat16 [512, 256, 128], P(('crops', 'dap')), parts along dimension 0
There are 2 independent parts, one for each index of `crops`. A program takes and returns all parts, laid end to end along the dimension named above; an argument that names none is the same for every part. Nothing has to cross between parts.
All inputs are finite; a program needn't handle non-finite values. No bound on the sum of `residue_mask` on one device may be relied on, other than what follows from the above.
Results may differ from a plain program's by a relative error of at most 0.0085.
Values may be sent and summed in bfloat16 or wider, within the bound.
A program may use at most 64 MiB of HBM per device.

v0:
```python
import math
import jax
import jax.numpy as jnp
from jax import lax
from jax.sharding import PartitionSpec as P


def side_by_side(arrays, axis, dim, along):
    widths = [math.prod(a.shape[along:]) for a in arrays]
    both = jnp.concatenate(
        [a.reshape(*a.shape[:along], w) for a, w in zip(arrays, widths)], axis=along
    )
    out = lax.all_gather(both, axis, axis=dim, tiled=True)
    blocks = jnp.split(out, [sum(widths[:k]) for k in range(1, len(widths))], axis=along)
    return tuple((b.reshape(*out.shape[:along], *a.shape[along:]) for a, b in zip(arrays, blocks)))


def in_order(blocks, dim):
    lengths = list(blocks.shape[1:])
    lengths[dim] *= blocks.shape[0]
    return jnp.moveaxis(blocks, 0, dim).reshape(lengths)


def copy_for_each(shard, axis):
    peers = lax.axis_size(axis)
    return lax.all_to_all(
        jnp.broadcast_to(shard[None], (peers, *shard.shape)), axis, 0, 0, tiled=True
    )


def gathered_copies(shard, axis, dim):
    return in_order(copy_for_each(shard, axis), dim)


def layer_norm(values, axis):
    center = values - jnp.mean(values, axis=axis, keepdims=True)
    spread = jnp.mean(center * center, axis=axis, keepdims=True)
    return center * lax.rsqrt(spread + 1e-05)


def gated_edges(projected, mask_block):
    masked = mask_block[:, :, None]
    first = (masked * jax.nn.sigmoid(projected[:, :, 1]) * projected[:, :, 0]).astype(jnp.bfloat16)
    second = (masked * jax.nn.sigmoid(projected[:, :, 3]) * projected[:, :, 2]).astype(jnp.bfloat16)
    return (jnp.transpose(first, (2, 0, 1)), jnp.transpose(second, (2, 0, 1)))


def body(
    prior_pair,
    single,
    target,
    residue_mask,
    recycle_gain,
    recycle_bias,
    left_single,
    right_single,
    left_target,
    right_target,
    tri_gain,
    tri_proj,
    tri_gate,
    tri_gate_bias,
    tri_out_gain,
    tri_out,
):
    row_count, col_count, depth = prior_pair.shape
    hidden_width = tri_proj.shape[3]
    mask_float = residue_mask.astype(jnp.float32)
    one_hot = (
        target[:, None] == jnp.arange(left_target.shape[0], dtype=jnp.int32)[None, :]
    ).astype(jnp.bfloat16)
    left_terms = jnp.dot(single, left_single, preferred_element_type=jnp.float32) + jnp.dot(
        one_hot, left_target, preferred_element_type=jnp.float32
    )
    right_terms = jnp.dot(single, right_single, preferred_element_type=jnp.float32) + jnp.dot(
        one_hot, right_target, preferred_element_type=jnp.float32
    )
    right_whole, mask_whole = side_by_side((right_terms, mask_float), "dap", 0, 1)
    pair_mask = mask_float[:, None] * mask_whole[None, :]
    prior_norm = layer_norm(prior_pair.astype(jnp.float32), 2) * recycle_gain + recycle_bias
    pair_state = (prior_norm + left_terms[:, None, :] + right_whole[None, :, :]).astype(
        jnp.bfloat16
    )
    groups = lax.axis_size("chan")
    member = lax.axis_index("chan")
    local_width = hidden_width // groups

    def local_edges(flat_normed, weights):
        weights_local = lax.dynamic_slice_in_dim(weights, member * local_width, local_width, 2)
        projected = jnp.dot(
            flat_normed,
            weights_local.reshape(depth, 4 * local_width),
            preferred_element_type=jnp.float32,
        )
        return gated_edges(projected.reshape(row_count, col_count, 4, local_width), pair_mask)

    for layer in range(2):
        normed = (layer_norm(pair_state.astype(jnp.float32), 2) * tri_gain[layer]).astype(
            jnp.bfloat16
        )
        flat_normed = normed.reshape(-1, depth)
        if layer == 0:
            outgoing_left_edges, outgoing_right_edges = local_edges(flat_normed, tri_proj[layer])
            product = jnp.einsum(
                "cik,cjk->cij",
                outgoing_left_edges,
                lax.all_gather(outgoing_right_edges, "dap", axis=1, tiled=True),
                preferred_element_type=jnp.float32,
            )
        else:
            left_edges, right_edges = local_edges(flat_normed, tri_proj[layer])
            transposed = lax.all_to_all(left_edges, "dap", split_axis=2, concat_axis=1, tiled=True)
            product = jnp.einsum(
                "cki,ckj->cij",
                transposed,
                lax.all_gather(right_edges, "dap", axis=1, tiled=True),
                preferred_element_type=jnp.float32,
            )
        full_product = gathered_copies(product.astype(jnp.bfloat16), "chan", 0)
        normed_hidden = (
            layer_norm(full_product.astype(jnp.float32), 0) * tri_out_gain[layer][:, None, None]
        ).astype(jnp.bfloat16)
        update = jnp.einsum(
            "cij,cd->ijd", normed_hidden, tri_out[layer], preferred_element_type=jnp.float32
        )
        gating = jax.nn.sigmoid(
            jnp.dot(flat_normed, tri_gate[layer], preferred_element_type=jnp.float32)
            + tri_gate_bias[layer]
        )
        pair_state = (
            pair_state.astype(jnp.float32) + gating.reshape(row_count, col_count, depth) * update
        ).astype(jnp.bfloat16)
    return pair_state


def solution(mesh):
    placed = (
        P(("crops", "dap"), None, None),
        P(("crops", "dap"), None),
        P(("crops", "dap")),
        P(("crops", "dap")),
        P(),
        P(),
        P(),
        P(),
        P(),
        P(),
        P(),
        P(),
        P(),
        P(),
        P(),
        P(),
    )
    return jax.shard_map(
        body, mesh=mesh, in_specs=placed, out_specs=P(("crops", "dap"), None, None), check_vma=False
    )
```

profile of v0, /device:TPU:33, one launch (start us, length us, event | category | flops | bytes accessed | tf_op | source)
XLA Modules:
  0.0 407.9 jit_solution(16664484103935328032)
XLA Ops:
  6.6 0.7 fusion.99
  7.3 0.1 copy.51
  7.4 0.8 fusion.102
  8.3 0.9 convolution_add_fusion.2
  9.2 97.4 %all-gather = f32[64,4,129]{2,1,0:T(4,128)S(1)} all-gather(f32[1,4,129]{2,1,0:T(4,128)S(1)} %maximum_bitcast_fusion), channel_id=1, replica_groups=mesh['crops'=2,'dap'=64,'chan'=4] {'dap'}, dimensions={0}, use_global_device_ids=true | all-gather | bytes 134160 | tf_op jit(solution)/shard_map/all_gather | solution.py:13
  106.6 0.1 reshape.173
  106.7 0.1 slice_reduce_fusion
  106.8 1.1 convert_reduce_fusion.3
  107.9 1.3 fusion.40
  109.2 1.0 fusion.101
  110.3 0.9 convolution_add_fusion.3
  111.2 1.5 convert_reduce_fusion
  112.7 0.4 fusion.31
  113.1 0.8 slice_bitcast_fusion.7
  113.8 1.1 fusion.98
  114.9 0.2 constant_dynamic-slice_fusion
  115.1 0.1 copy.80
  115.2 0.3 fusion.33
  115.6 0.2 fusion.46
  115.9 0.7 fusion.81
  116.8 0.1 copy.85
  116.9 121.3 %all-gather.4.cloned.1.call-done = bf16[32,256,256]{2,0,1:T(8,128)(2,1)} async-done(((bf16[32,4,256]{2,0,1:T(8,128)(2,1)}), bf16[32,256,256]{2,0,1:T(8,128)(2,1)}) %all-gather.4.cloned.1.call-update) | async-done | bytes 4194320 | tf_op jit(solution)/shard_map/all_gather | solution.py:107
  238.2 4.5 %fusion.17 = bf16[32,4,256]{2,1,0:T(4,128)(2,1)S(1)} fusion(bf16[32,256,256]{2,0,1:T(8,128)(2,1)} %all-gather.4.cloned.1.call-done, bf16[32,4,256]{2,0,1:T(8,128)(2,1)S(1)} %get-tuple-element.11), kind=kOutput, calls=%fused_computation.21 | convolution fusion | flops 16809984 | bytes 4325376 | tf_op jit(solution)/shard_map/cik,cjk->cij/dot_general | solution.py:104
  242.8 0.7 broadcast_in_dim.4
  243.5 4.0 all-to-all-start
  247.5 0.3 fusion.9
  247.8 5.6 %all-to-all-done = bf16[4,32,4,256]{3,1,2,0:T(8,128)(2,1)S(1)} async-done(((bf16[4,32,4,256]{3,1,2,0:T(8,128)(2,1)}), bf16[4,32,4,256]{3,1,2,0:T(8,128)(2,1)S(1)}, u32[]{:S(2)}, u32[]{:S(2)}) %all-to-all-start) | async-done | bytes 262176 | tf_op jit(solution)/shard_map/all_to_all | solution.py:26
  253.5 0.1 fusion.39
  253.7 0.4 fusion.100
  254.1 0.4 multiply_reduce_fusion
  254.5 0.3 multiply_convert_fusion
  254.8 0.2 fusion.48
  255.1 0.7 fusion.84
  255.8 0.2 copy.64
  256.0 0.8 reshape.193
  256.8 14.6 %all-to-all-start.1 = ((bf16[64,2,256]{2,1,0:T(2,128)(2,1)}), bf16[64,2,256]{2,1,0:T(2,128)(2,1)S(1)}, u32[]{:S(2)}, u32[]{:S(2)}) async-start(bf16[64,2,256]{2,1,0:T(2,128)(2,1)} %reshape.193), calls=%async_computation.1 | async-start | bytes 131072 | tf_op jit(solution)/shard_map/all_to_all | solution.py:112
  271.6 24.9 %all-to-all-done.1 = bf16[64,2,256]{2,1,0:T(2,128)(2,1)S(1)} async-done(((bf16[64,2,256]{2,1,0:T(2,128)(2,1)}), bf16[64,2,256]{2,1,0:T(2,128)(2,1)S(1)}, u32[]{:S(2)}, u32[]{:S(2)}) %all-to-all-start.1) | async-done | bytes 65568 | tf_op jit(solution)/shard_map/all_to_all | solution.py:112
  296.5 0.2 reshape.194
  296.7 0.2 copy.66
  296.9 0.1 copy.69
  297.1 87.5 %all-gather.6.cloned.1.call-done = bf16[32,256,256]{2,0,1:T(8,128)(2,1)} async-done(((bf16[32,4,256]{2,0,1:T(8,128)(2,1)}), bf16[32,256,256]{2,0,1:T(8,128)(2,1)}) %all-gather.6.cloned.1.call-update) | async-done | bytes 4194320 | tf_op jit(solution)/shard_map/all_gather | solution.py:116
  384.6 4.5 %fusion.20 = bf16[32,4,256]{2,1,0:T(4,128)(2,1)S(1)} fusion(bf16[32,256,4]{1,2,0:T(4,128)(2,1)S(1)} %copy.69, bf16[32,256,256]{2,0,1:T(8,128)(2,1)} %all-gather.6.cloned.1.call-done), kind=kOutput, calls=%fused_computation.22 | convolution fusion | flops 16809984 | bytes 4325376 | tf_op jit(solution)/shard_map/cki,ckj->cij/dot_general | solution.py:113
  389.1 0.7 broadcast_in_dim.5
  389.9 4.1 all-to-all-start.2
  393.9 0.3 fusion.12
  394.2 5.6 %all-to-all-done.2 = bf16[4,32,4,256]{3,1,2,0:T(8,128)(2,1)S(1)} async-done(((bf16[4,32,4,256]{3,1,2,0:T(8,128)(2,1)}), bf16[4,32,4,256]{3,1,2,0:T(8,128)(2,1)S(1)}, u32[]{:S(2)}, u32[]{:S(2)}) %all-to-all-start.2) | async-done | bytes 262176 | tf_op jit(solution)/shard_map/all_to_all | solution.py:26
  400.0 0.1 fusion.36
  400.1 1.0 fusion.14
  (38 shorter events, 0.9 us)
Async XLA Ops:
  6.5 0.9 copy-start
  6.6 110.1 %copy-start.2 = (f32[2,128]{1,0:T(2,128)S(1)}, f32[2,128]{1,0:T(2,128)}, u32[]{:S(2)}) copy-start(f32[2,128]{1,0:T(2,128)} %param.30) | copy-start | bytes 3076
  6.6 110.3 %copy-start.3 = (f32[2,128]{1,0:T(2,128)S(1)}, f32[2,128]{1,0:T(2,128)}, u32[]{:S(2)}) copy-start(f32[2,128]{1,0:T(2,128)} %param.29) | copy-start | bytes 3076
  6.6 231.6 %all-gather.4.cloned.1.call-start = ((), (), s32[]{:S(2)}) async-start(), calls=%async_computation.3 | async-start | bytes 4259840 | tf_op jit(solution)/shard_map/all_gather | solution.py:107
  114.9 132.6 %copy-start.4 = (bf16[2,128,128]{2,1,0:T(8,128)(2,1)S(1)}, bf16[2,128,128]{2,1,0:T(8,128)(2,1)}, u32[]{:S(2)}) copy-start(bf16[2,128,128]{2,1,0:T(8,128)(2,1)} %param.28) | copy-start | bytes 196612
  238.2 15.5 %copy-start.1 = (bf16[2,128,128]{2,1,0:T(8,128)(2,1)S(1)}, bf16[2,128,128]{2,1,0:T(8,128)(2,1)}, u32[]{:S(2)}) copy-start(bf16[2,128,128]{2,1,0:T(8,128)(2,1)} %param.31) | copy-start | bytes 196612
  243.5 9.9 %all-to-all-start = ((bf16[4,32,4,256]{3,1,2,0:T(8,128)(2,1)}), bf16[4,32,4,256]{3,1,2,0:T(8,128)(2,1)S(1)}, u32[]{:S(2)}, u32[]{:S(2)}) async-start(bf16[4,32,4,256]{3,1,2,0:T(8,128)(2,1)} %broadcast_in_dim.4), calls=%async_computation | async-start | bytes 524288 | tf_op jit(solution)/shard_map/all_to_all | solution.py:26
  247.5 137.1 %all-gather.6.cloned.1.call-start = ((), (), s32[]{:S(2)}) async-start(), calls=%async_computation.4 | async-start | bytes 4259840 | tf_op jit(solution)/shard_map/all_gather | solution.py:116
  256.8 39.6 %all-to-all-start.1 = ((bf16[64,2,256]{2,1,0:T(2,128)(2,1)}), bf16[64,2,256]{2,1,0:T(2,128)(2,1)S(1)}, u32[]{:S(2)}, u32[]{:S(2)}) async-start(bf16[64,2,256]{2,1,0:T(2,128)(2,1)} %reshape.193), calls=%async_computation.1 | async-start | bytes 131072 | tf_op jit(solution)/shard_map/all_to_all | solution.py:112
  389.9 10.0 %all-to-all-start.2 = ((bf16[4,32,4,256]{3,1,2,0:T(8,128)(2,1)}), bf16[4,32,4,256]{3,1,2,0:T(8,128)(2,1)S(1)}, u32[]{:S(2)}, u32[]{:S(2)}) async-start(bf16[4,32,4,256]{3,1,2,0:T(8,128)(2,1)} %broadcast_in_dim.5), calls=%async_computation.2 | async-start | bytes 524288 | tf_op jit(solution)/shard_map/all_to_all | solution.py:26
Sparse Core Ops, SparseCore 0:
  116.8 121.3 all-gather.3
  255.9 128.6 all-gather.5
where the time goes:
time: 409 us; the launch traced here: 408 us
  waiting for transfers between devices  245 us (60%)
  blocking collectives  97.4 us (24%)
  starting transfers between devices  22.7 us (6%)
  matrix products  15.1 us (4%)
  between operations  13.7 us (3%)
  other arithmetic  8.15 us (2%)
  local copies, waits for them, and re-layouts  5.89 us (1%)
    all_gather x1, waiting for transfers between devices, body(): lax.all_gather(outgoing_right_edges, 'dap', axis=1, tiled=True)  121 us
    all_gather x1, blocking collectives, side_by_side(): out = lax.all_gather(both, axis, axis=dim, tiled=True)  97.4 us
    all_gather x1, waiting for transfers between devices, body(): lax.all_gather(right_edges, 'dap', axis=1, tiled=True)  87.5 us
    all_to_all x1, waiting for transfers between devices, body(): lax.all_to_all(left_edges, 'dap', split_axis=2, concat_axis=1, tiled=True)  24.9 us
    all_to_all x1, starting transfers between devices, body(): lax.all_to_all(left_edges, 'dap', split_axis=2, concat_axis=1, tiled=True)  14.6 us
    all_to_all x2, waiting for transfers between devices, copy_for_each(): lax.all_to_all(jnp.broadcast_to(shard[None], (peers, *shard.shape)), axis...  11.2 us
  transfers between devices with their start and end apart: 5, of which 5 were waited for; matrix products, arithmetic and copies ran while one was open for 1% of the time, Pallas kernels for 0%

commit v1 on v0

--- a/solution.py
+++ b/solution.py
@@ -1,8 +1,21 @@
+import functools
 import math
 import jax
 import jax.numpy as jnp
 from jax import lax
 from jax.sharding import PartitionSpec as P
+from jax.lax import all_to_all, axis_size
+
+
+def meet_the_loops(panel, ndim_at):
+    lower = jnp.concatenate(
+        all_to_all(jnp.stack([panel for _ in range(axis_size("dap"))], axis=0), "dap", 0, 0),
+        axis=ndim_at,
+    )
+    return lower
+
+
+put_slot_in = functools.partial(meet_the_loops, ndim_at=1)
 
 
 def side_by_side(arrays, axis, dim, along):
@@ -104,7 +117,7 @@
             product = jnp.einsum(
                 "cik,cjk->cij",
                 outgoing_left_edges,
-                lax.all_gather(outgoing_right_edges, "dap", axis=1, tiled=True),
+                put_slot_in(outgoing_right_edges),
                 preferred_element_type=jnp.float32,
             )
         else:

time: 409 us -> 681 us (1.67)
  waiting for transfers between devices: 245 us -> 495 us
  local copies, waits for them, and re-layouts: 5.89 us -> 23.2 us
    all_to_all x0 -> x1, waiting for transfers between devices: none -> 372 us  [meet_the_loops(): all_to_all(jnp.stack([panel for _ in range(axis_size('dap'))], axis=0), '...]
    all_gather x1 -> x0, waiting for transfers between devices: 121 us -> none  [body(): lax.all_gather(outgoing_right_edges, 'dap', axis=1, tiled=True)]
    reshape x0 -> x2, local copies, waits for them, and re-layouts: none -> 13.3 us  [meet_the_loops(): jnp.concatenate(all_to_all(jnp.stack([panel for _ in range(axis_size('dap...]
  transfers between devices with their start and end apart: 5 -> 5, of which waited for: 5 -> 5; matrix products, arithmetic and copies ran while one was open for 1% -> 0% of each run, Pallas kernels for 0% -> 0%
where the time goes in v1:
time: 681 us; the launch traced here: 680 us
  waiting for transfers between devices  495 us (73%)
  blocking collectives  97.4 us (14%)
  starting transfers between devices  28.8 us (4%)
  local copies, waits for them, and re-layouts  23.2 us (3%)
  matrix products  13.9 us (2%)
  between operations  13.7 us (2%)
  other arithmetic  7.52 us (1%)
    all_to_all x1, waiting for transfers between devices, meet_the_loops(): all_to_all(jnp.stack([panel for _ in range(axis_size('dap'))], axis=0), '...  372 us
    all_gather x1, blocking collectives, side_by_side(): out = lax.all_gather(both, axis, axis=dim, tiled=True)  97.4 us
    all_gather x1, waiting for transfers between devices, body(): lax.all_gather(right_edges, 'dap', axis=1, tiled=True)  85.9 us
    all_to_all x1, waiting for transfers between devices, body(): lax.all_to_all(left_edges, 'dap', split_axis=2, concat_axis=1, tiled=True)  26.7 us
    all_to_all x1, starting transfers between devices, body(): lax.all_to_all(left_edges, 'dap', split_axis=2, concat_axis=1, tiled=True)  14.7 us
  transfers between devices with their start and end apart: 5, of which 5 were waited for; matrix products, arithmetic and copies ran while one was open for 0% of the time, Pallas kernels for 0%

profile of v1, /device:TPU:33, one launch (start us, length us, event | category | flops | bytes accessed | tf_op | source)
XLA Modules:
  0.0 679.8 jit_solution(3352724007458941109)
XLA Ops:
  6.6 0.7 fusion.94
  7.3 0.1 copy-done
  7.5 0.8 fusion.97
  8.3 0.9 convolution_add_fusion.2
  9.2 97.4 %all-gather = f32[64,4,129]{2,1,0:T(4,128)S(1)} all-gather(f32[1,4,129]{2,1,0:T(4,128)S(1)} %maximum_bitcast_fusion), channel_id=1, replica_groups=mesh['crops'=2,'dap'=64,'chan'=4] {'dap'}, dimensions={0}, use_global_device_ids=true | all-gather | bytes 134160 | tf_op jit(solution)/shard_map/all_gather | solution.py:26
  106.7 0.1 slice_reduce_fusion
  106.8 1.1 convert_reduce_fusion.3
  107.9 1.3 fusion.35
  109.2 1.0 fusion.96
  110.3 0.9 convolution_add_fusion.3
  111.2 1.5 convert_reduce_fusion
  112.7 0.4 fusion.26
  113.1 0.8 slice_bitcast_fusion.7
  113.9 1.1 fusion.93
  114.9 0.2 constant_dynamic-slice_fusion
  115.2 0.3 fusion.28
  115.6 0.2 fusion.41
  116.0 4.0 stack.2
  120.0 6.2 all-to-all-start
  126.5 371.8 %all-to-all-done = bf16[64,32,4,256]{3,2,1,0:T(4,128)(2,1)} async-done(((bf16[64,32,4,256]{3,2,1,0:T(4,128)(2,1)}), bf16[64,32,4,256]{3,2,1,0:T(4,128)(2,1)}, u32[]{:S(2)}, u32[]{:S(2)}) %all-to-all-start) | async-done | bytes 4194336 | tf_op jit(solution)/shard_map/all_to_all | solution.py:12
  498.3 6.3 copy.57
  504.6 6.9 %reshape.178 = bf16[32,256,256]{2,1,0:T(8,128)(2,1)} reshape(bf16[32,64,4,256]{3,2,1,0:T(4,128)(2,1)} %copy.57) | data formatting | bytes 8388608 | tf_op jit(solution)/shard_map/reshape | solution.py:11
  511.5 3.4 convolution_convert_fusion
  515.0 0.7 broadcast_in_dim.4
  515.7 4.3 all-to-all-start.1
  520.0 0.3 fusion.7
  520.3 5.2 all-to-all-done.1
  525.7 0.1 fusion.34
  525.8 0.4 fusion.95
  526.2 0.4 multiply_reduce_fusion
  526.6 0.3 multiply_convert_fusion
  527.0 0.2 fusion.43
  527.2 0.7 fusion.79
  528.0 0.2 copy.65
  528.2 0.8 reshape.203
  529.0 14.7 %all-to-all-start.2 = ((bf16[64,2,256]{2,1,0:T(2,128)(2,1)}), bf16[64,2,256]{2,1,0:T(2,128)(2,1)S(1)}, u32[]{:S(2)}, u32[]{:S(2)}) async-start(bf16[64,2,256]{2,1,0:T(2,128)(2,1)} %reshape.203), calls=%async_computation.2 | async-start | bytes 131072 | tf_op jit(solution)/shard_map/all_to_all | solution.py:125
  543.8 26.7 %all-to-all-done.2 = bf16[64,2,256]{2,1,0:T(2,128)(2,1)S(1)} async-done(((bf16[64,2,256]{2,1,0:T(2,128)(2,1)}), bf16[64,2,256]{2,1,0:T(2,128)(2,1)S(1)}, u32[]{:S(2)}, u32[]{:S(2)}) %all-to-all-start.2) | async-done | bytes 65568 | tf_op jit(solution)/shard_map/all_to_all | solution.py:125
  570.5 0.2 reshape.204
  570.7 0.2 copy.67
  571.0 0.1 copy.70
  571.1 85.9 %all-gather.3.cloned.1.call-done = bf16[32,256,256]{2,0,1:T(8,128)(2,1)} async-done(((bf16[32,4,256]{2,0,1:T(8,128)(2,1)}), bf16[32,256,256]{2,0,1:T(8,128)(2,1)}) %all-gather.3.cloned.1.call-update) | async-done | bytes 4194320 | tf_op jit(solution)/shard_map/all_gather | solution.py:129
  657.0 4.5 fusion.15
  661.5 0.7 broadcast_in_dim.5
  662.3 3.5 all-to-all-start.3
  665.8 0.3 fusion.10
  666.1 5.6 all-to-all-done.3
  671.9 0.1 fusion.31
  672.0 1.0 fusion.12
  (41 shorter events, 1.3 us)
Async XLA Ops:
  6.5 0.9 copy-start
  120.0 6.2 copy-start.2
  120.0 6.4 copy-start.3
  120.0 378.2 %all-to-all-start = ((bf16[64,32,4,256]{3,2,1,0:T(4,128)(2,1)}), bf16[64,32,4,256]{3,2,1,0:T(4,128)(2,1)}, u32[]{:S(2)}, u32[]{:S(2)}) async-start(bf16[64,32,4,256]{3,2,1,0:T(4,128)(2,1)} %stack.2), calls=%async_computation | async-start | bytes 8388608 | tf_op jit(solution)/shard_map/all_to_all | solution.py:12
  511.5 8.5 %copy-start.4 = (bf16[2,128,128]{2,1,0:T(8,128)(2,1)S(1)}, bf16[2,128,128]{2,1,0:T(8,128)(2,1)}, u32[]{:S(2)}) copy-start(bf16[2,128,128]{2,1,0:T(8,128)(2,1)} %param.28) | copy-start | bytes 196612
  511.5 14.3 %copy-start.1 = (bf16[2,128,128]{2,1,0:T(8,128)(2,1)S(1)}, bf16[2,128,128]{2,1,0:T(8,128)(2,1)}, u32[]{:S(2)}) copy-start(bf16[2,128,128]{2,1,0:T(8,128)(2,1)} %param.31) | copy-start | bytes 196612
  515.7 9.8 %all-to-all-start.1 = ((bf16[4,32,4,256]{3,1,2,0:T(8,128)(2,1)}), bf16[4,32,4,256]{3,1,2,0:T(8,128)(2,1)S(1)}, u32[]{:S(2)}, u32[]{:S(2)}) async-start(bf16[4,32,4,256]{3,1,2,0:T(8,128)(2,1)} %broadcast_in_dim.4), calls=%async_computation.1 | async-start | bytes 524288 | tf_op jit(solution)/shard_map/all_to_all | solution.py:39
  520.0 137.0 %all-gather.3.cloned.1.call-start = ((), (), s32[]{:S(2)}) async-start(), calls=%async_computation.4 | async-start | bytes 4259840 | tf_op jit(solution)/shard_map/all_gather | solution.py:129
  529.0 41.5 %all-to-all-start.2 = ((bf16[64,2,256]{2,1,0:T(2,128)(2,1)}), bf16[64,2,256]{2,1,0:T(2,128)(2,1)S(1)}, u32[]{:S(2)}, u32[]{:S(2)}) async-start(bf16[64,2,256]{2,1,0:T(2,128)(2,1)} %reshape.203), calls=%async_computation.2 | async-start | bytes 131072 | tf_op jit(solution)/shard_map/all_to_all | solution.py:125
  662.3 9.4 %all-to-all-start.3 = ((bf16[4,32,4,256]{3,1,2,0:T(8,128)(2,1)}), bf16[4,32,4,256]{3,1,2,0:T(8,128)(2,1)S(1)}, u32[]{:S(2)}, u32[]{:S(2)}) async-start(bf16[4,32,4,256]{3,1,2,0:T(8,128)(2,1)} %broadcast_in_dim.5), calls=%async_computation.3 | async-start | bytes 524288 | tf_op jit(solution)/shard_map/all_to_all | solution.py:39
Sparse Core Ops, SparseCore 0:
  528.1 128.8 all-gather.2
